TPU v7x, 256 devices: a whole 4x4x8 slice. The times are simulated.
256 devices in a mesh: gx: 16 (over z, x_lo), gy: 16 (over y, x_hi, core).
Axes of the slice: x: 4 (x_hi: 2, x_lo: 2; x = x_hi * 2 + x_lo), y: 4, z: 8, core: 2. Of those that a mesh axis runs over, the one named last changes fastest.
Arguments:
- gradient: float32 [2048, 512], P('gx', 'gy'), may hold values from -6 to 6
- stat_old: float32 [2048, 2048], P('gx', 'gy'), may hold values from -1.001 to 1.001, as said below
Outputs:
- statistic: float32 [2048, 2048], P('gx', 'gy')
- inverse_root: float32 [2048, 2048], P('gx', 'gy')
Inputs may be any that keep to these rules, and one draw needn't show every extreme that they name: stat_old is symmetric positive semidefinite with unit diagonal, the Gram matrix of 2048 unit-length rows of 512 entries.
All inputs are finite; a program needn't handle non-finite values.
Results may differ from a plain program's by a relative error of at most 0.0003.
Values sent between devices are 32-bit elements.
A program may use at most 64 MiB of HBM per device.

v0:
```python
import jax
import jax.numpy as jnp
from jax import lax
from jax.sharding import Mesh
from jax.sharding import PartitionSpec as P

GY = ("gy_0", "gy_1", "gy_2")
GX = ("gx_0", "gx_1")
GX_GY = ("gx_0", "gx_1", "gy_0", "gy_1", "gy_2")


def gather_axes(array, axes, dim):
    filled = array
    for number in range(len(axes) - 1, -1, -1):
        filled = lax.all_gather(filled, axes[number], axis=dim, tiled=True)
    return filled


def folded(array, axes, dim, take_in, carry):
    everything = jax.tree.map(lambda part: gather_axes(part, axes, dim), array)
    return take_in(carry, everything, jnp.int32(0))


def spread(array, axes, root):
    array = jnp.where(lax.axis_index(axes) == root, array, jnp.zeros_like(array))
    for axis in axes:
        array = lax.psum(array, axis)
    return array


def over_axes(array, axes):
    for axis in axes:
        array = lax.psum(array, axis)
    return array


def matmul(leading, trailing):
    return jnp.dot(
        leading, trailing, preferred_element_type=jnp.float32, precision=lax.Precision.HIGHEST
    )


def panels(factor_one, factor_two):
    whole_row = lax.all_gather(factor_one, GY, axis=1, tiled=True)

    def accumulate(running, shard_rows, first_row):
        matching = lax.dynamic_slice_in_dim(whole_row, first_row, shard_rows.shape[0], 1)
        return running + matmul(matching, shard_rows)

    empty = jnp.zeros((factor_one.shape[0], factor_two.shape[1]), jnp.float32)
    return folded(factor_two, GX, 0, accumulate, empty)


def product(factor_one, factor_two):
    return panels(factor_one, factor_two)


def local(gradient, stat_old):
    count_rows = lax.axis_size(GX)
    count_cols = lax.axis_size(GY)
    factor = count_rows // count_cols
    piece_width = stat_old.shape[0]
    row_index = lax.axis_index(GX)
    col_index = lax.axis_index(GY)
    panel_rows = lax.all_gather(gradient, GY, axis=1, tiled=True)
    outer_parts = []
    for member in range(factor):
        column_rows = spread(panel_rows, GX, col_index * factor + member)
        outer_parts.append(matmul(panel_rows, column_rows.T))
    outer = jnp.concatenate(outer_parts, axis=1) / panel_rows.shape[1]
    statistic = 0.9 * stat_old + outer
    squares = over_axes(jnp.sum(statistic * statistic), GX_GY)
    divisor = 2.0 * jnp.sqrt(squares / (piece_width * count_rows))
    global_rows = row_index * piece_width + lax.broadcasted_iota(jnp.int32, stat_old.shape, 0)
    global_cols = col_index * (factor * piece_width) + lax.broadcasted_iota(
        jnp.int32, stat_old.shape, 1
    )
    identity = (global_rows == global_cols).astype(jnp.float32)
    normed = statistic / divisor
    first_step = 1.5 * identity - 0.5 * normed
    root_half = product(normed, first_step)
    product_mid = product(first_step, root_half)
    second_step = 1.5 * identity - 0.5 * product_mid
    inverse_root = product(second_step, first_step)
    return (statistic, inverse_root)


def solution(mesh):
    torus = Mesh(mesh.devices.reshape(8, 2, 4, 2, 2), ("gx_0", "gx_1", "gy_0", "gy_1", "gy_2"))
    placed = (P(GX, GY), P(GX, GY))
    return jax.shard_map(
        local, mesh=torus, in_specs=placed, out_specs=(P(GX, GY), P(GX, GY)), check_vma=False
    )
```

profile of v0, /device:TPU:1, one launch (start us, length us, event | category | flops | bytes accessed | tf_op | source)
XLA Modules:
  0.0 435.5 jit_solution(8363940582427046131)
XLA Ops:
  7.2 0.7 copy-done.3
  7.9 26.8 %all_gather.26 = f32[128,512]{0,1:T(8,128)S(1)} all-gather(f32[128,32]{0,1:T(8,128)S(1)} %copy-done.3), channel_id=1, replica_groups=mesh['gx_0'=8,'gx_1'=2,'gy_0'=4,'gy_1'=2,'gy_2'=2] {'gy_0','gy_1','gy_2'}, dimensions={1}, use_global_device_ids=true | all-gather | bytes 278528 | tf_op jit(solution)/shard_map/all_gather | solution.py:65
  34.6 0.7 broadcast_select_fusion
  35.4 65.4 %all-reduce.3.cloned.1.call-done = f32[128,512]{0,1:T(8,128)} async-done(((f32[128,512]{0,1:T(8,128)}), f32[128,512]{0,1:T(8,128)}) %all-reduce.3.cloned.1.call-update) | async-done | bytes 262160 | tf_op jit(solution)/shard_map/psum | solution.py:27
  100.9 0.8 copy-done.2
  101.7 39.7 %all-reduce.5.cloned.1.call-done = f32[128,512]{0,1:T(8,128)} async-done(((f32[128,512]{0,1:T(8,128)}), f32[128,512]{0,1:T(8,128)}) %all-reduce.5.cloned.1.call-update) | async-done | bytes 262160 | tf_op jit(solution)/shard_map/psum | solution.py:27
  141.4 2.1 multiply_reduce_fusion
  143.6 14.6 %psum.51 = f32[]{:T(128)} all-reduce(f32[]{:T(128)} %get-tuple-element.6), channel_id=1, replica_groups=mesh['gx_0'=8,'gx_1'=2,'gy_0'=4,'gy_1'=2,'gy_2'=2] {'gx_0'}, use_global_device_ids=true, to_apply=%region_3.4 | all-reduce | flops 1 | bytes 8 | tf_op jit(solution)/shard_map/psum | solution.py:33
  158.1 4.4 %psum.52 = f32[]{:T(128)} all-reduce(f32[]{:T(128)} %psum.51), channel_id=1, replica_groups=mesh['gx_0'=8,'gx_1'=2,'gy_0'=4,'gy_1'=2,'gy_2'=2] {'gx_1'}, use_global_device_ids=true, to_apply=%region_4.5 | all-reduce | flops 1 | bytes 8 | tf_op jit(solution)/shard_map/psum | solution.py:33
  162.5 9.1 %psum.53 = f32[]{:T(128)} all-reduce(f32[]{:T(128)} %psum.52), channel_id=1, replica_groups=mesh['gx_0'=8,'gx_1'=2,'gy_0'=4,'gy_1'=2,'gy_2'=2] {'gy_0'}, use_global_device_ids=true, to_apply=%region_5.6 | all-reduce | flops 1 | bytes 8 | tf_op jit(solution)/shard_map/psum | solution.py:33
  171.6 5.9 %psum.54 = f32[]{:T(128)} all-reduce(f32[]{:T(128)} %psum.53), channel_id=1, replica_groups=mesh['gx_0'=8,'gx_1'=2,'gy_0'=4,'gy_1'=2,'gy_2'=2] {'gy_1'}, use_global_device_ids=true, to_apply=%region_6.7 | all-reduce | flops 1 | bytes 8 | tf_op jit(solution)/shard_map/psum | solution.py:33
  177.5 11.8 %psum.55 = f32[]{:T(128)} all-reduce(f32[]{:T(128)} %psum.54), channel_id=1, replica_groups=mesh['gx_0'=8,'gx_1'=2,'gy_0'=4,'gy_1'=2,'gy_2'=2] {'gy_2'}, use_global_device_ids=true, to_apply=%region_7.8 | all-reduce | flops 1 | bytes 8 | tf_op jit(solution)/shard_map/psum | solution.py:33
  190.0 0.6 select_subtract_fusion
  190.6 3.9 all_gather.29
  195.7 29.4 %all-gather.10.cloned.1.call-done = f32[2048,128]{0,1:T(8,128)} async-done(((f32[256,128]{0,1:T(8,128)}), f32[2048,128]{0,1:T(8,128)}) %all-gather.10.cloned.1.call-update) | async-done | bytes 1048592 | tf_op jit(solution)/shard_map/all_gather | solution.py:15
  225.1 56.8 %all-gather.8.cloned.1.call-done = f32[128,2048]{0,1:T(8,128)} async-done(((f32[128,128]{0,1:T(8,128)}), f32[128,2048]{0,1:T(8,128)}) %all-gather.8.cloned.1.call-update) | async-done | bytes 1048592 | tf_op jit(solution)/shard_map/all_gather | solution.py:44
  281.9 3.4 fusion.3
  285.2 3.9 all_gather.31
  289.2 44.5 %all-gather.6.cloned.1.call-done = f32[128,2048]{0,1:T(8,128)} async-done(((f32[128,128]{0,1:T(8,128)}), f32[128,2048]{0,1:T(8,128)}) %all-gather.6.cloned.1.call-update) | async-done | bytes 1048592 | tf_op jit(solution)/shard_map/all_gather | solution.py:44
  333.7 33.6 %all-gather.12.cloned.1.call-done = f32[2048,128]{1,0:T(8,128)} async-done(((f32[256,128]{1,0:T(8,128)}), f32[2048,128]{1,0:T(8,128)}) %all-gather.12.cloned.1.call-update) | async-done | bytes 1048592 | tf_op jit(solution)/shard_map/all_gather | solution.py:15
  367.3 4.0 fusion
  371.3 0.7 copy.5
  372.0 53.0 %all-gather.14.cloned.1.call-done = f32[128,2048]{0,1:T(8,128)} async-done(((f32[128,128]{0,1:T(8,128)}), f32[128,2048]{0,1:T(8,128)}) %all-gather.14.cloned.1.call-update) | async-done | bytes 1048592 | tf_op jit(solution)/shard_map/all_gather | solution.py:44
  425.0 3.7 fusion.4
  (22 shorter events, 1.5 us)
Async XLA Ops:
  7.2 0.7 copy-start.3
  7.2 93.6 %all-reduce.3.cloned.1.call-start = ((), (), s32[]{:S(2)}) async-start(), calls=%async_computation | async-start | bytes 524288 | tf_op jit(solution)/shard_map/psum | solution.py:27
  35.4 106.1 %all-reduce.5.cloned.1.call-start = ((), (), s32[]{:S(2)}) async-start(), calls=%async_computation.1 | async-start | bytes 524288 | tf_op jit(solution)/shard_map/psum | solution.py:27
  100.8 0.8 copy-start.2
  100.8 124.2 %all-gather.10.cloned.1.call-start = ((), (), s32[]{:S(2)}) async-start(), calls=%async_computation.4 | async-start | bytes 1179648 | tf_op jit(solution)/shard_map/all_gather | solution.py:15
  190.6 3.9 copy-start.1
  194.5 87.3 %all-gather.8.cloned.1.call-start = ((), (), s32[]{:S(2)}) async-start(), calls=%async_computation.3 | async-start | bytes 1114112 | tf_op jit(solution)/shard_map/all_gather | solution.py:44
  195.1 138.6 %all-gather.6.cloned.1.call-start = ((), (), s32[]{:S(2)}) async-start(), calls=%async_computation.2 | async-start | bytes 1114112 | tf_op jit(solution)/shard_map/all_gather | solution.py:44
  195.7 171.6 %all-gather.12.cloned.1.call-start = ((), (), s32[]{:S(2)}) async-start(), calls=%async_computation.5 | async-start | bytes 1179648 | tf_op jit(solution)/shard_map/all_gather | solution.py:15
  289.1 135.9 %copy-start = (f32[2048,128]{0,1:T(8,128)S(1)}, f32[2048,128]{0,1:T(8,128)}, u32[]{:S(2)}) copy-start(f32[2048,128]{0,1:T(8,128)} %all-gather.10.cloned.1.call-done) | copy-start | bytes 3145732
  289.1 135.9 %all-gather.14.cloned.1.call-start = ((), (), s32[]{:S(2)}) async-start(), calls=%async_computation.6 | async-start | bytes 1114112 | tf_op jit(solution)/shard_map/all_gather | solution.py:44
Sparse Core Ops, SparseCore 0:
  35.5 65.2 all-reduce.2
  103.4 38.0 all-reduce.4
  194.6 30.4 all-gather.9
  228.3 53.5 all-gather.7
  285.0 48.6 all-gather.5
  335.4 31.8 all-gather.11
  371.4 53.5 all-gather.13
where the time goes:
time: 436 us
  waiting for transfers between devices  323 us (74%)
  blocking collectives  80.2 us (18%)
  between operations  14.9 us (3%)
  matrix products  13.2 us (3%)
    all_gather x3, waiting for transfers between devices, panels(): whole_row = lax.all_gather(factor_one, GY, axis=1, tiled=True)  154 us
    psum x2, waiting for transfers between devices, spread(): array = lax.psum(array, axis)  105 us
    all_gather x2, waiting for transfers between devices, gather_axes(): filled = lax.all_gather(filled, axes[number], axis=dim, tiled=True)  62.9 us
    psum x5, blocking collectives, over_axes(): array = lax.psum(array, axis)  45.7 us
    all_gather x1, blocking collectives, local(): panel_rows = lax.all_gather(gradient, GY, axis=1, tiled=True)  26.8 us
    dot_general x4, matrix products, matmul(): jnp.dot(leading, trailing, preferred_element_type=jnp.float32, precision=...  13.2 us
  transfers between devices with their start and end apart: 7, of which 7 were waited for; matrix products, arithmetic and copies ran while one was open for 1% of the time, Pallas kernels for 0%

commit v1 on v0

--- a/solution.py
+++ b/solution.py
@@ -62,7 +62,7 @@
     piece_width = stat_old.shape[0]
     row_index = lax.axis_index(GX)
     col_index = lax.axis_index(GY)
-    panel_rows = lax.all_gather(gradient, GY, axis=1, tiled=True)
+    panel_rows = jnp.concatenate(lax.all_gather(gradient, GY), axis=1)
     outer_parts = []
     for member in range(factor):
         column_rows = spread(panel_rows, GX, col_index * factor + member)

time: 436 us -> 436 us (level)
  no operation moved by 1% of the time
where the time goes in v1:
time: 436 us
  waiting for transfers between devices  323 us (74%)
  blocking collectives  80.2 us (18%)
  between operations  14.9 us (3%)
  matrix products  13.2 us (3%)
    all_gather x3, waiting for transfers between devices, panels(): whole_row = lax.all_gather(factor_one, GY, axis=1, tiled=True)  154 us
    psum x2, waiting for transfers between devices, spread(): array = lax.psum(array, axis)  105 us
    all_gather x2, waiting for transfers between devices, gather_axes(): filled = lax.all_gather(filled, axes[number], axis=dim, tiled=True)  62.9 us
    psum x5, blocking collectives, over_axes(): array = lax.psum(array, axis)  45.7 us
    all_gather x1, blocking collectives, local(): panel_rows = jnp.concatenate(lax.all_gather(gradient, GY), axis=1)  26.8 us
    dot_general x4, matrix products, matmul(): jnp.dot(leading, trailing, preferred_element_type=jnp.float32, precision=...  13.2 us
  transfers between devices with their start and end apart: 7, of which 7 were waited for; matrix products, arithmetic and copies ran while one was open for 1% of the time, Pallas kernels for 0%

profile of v1, /device:TPU:1, one launch (start us, length us, event | category | flops | bytes accessed | tf_op | source)
XLA Modules:
  0.0 435.7 jit_solution(8314178923199854298)
XLA Ops:
  7.2 0.7 copy-done.3
  7.9 26.8 %all-gather = f32[2048,32]{0,1:T(8,128)S(1)} all-gather(f32[128,32]{0,1:T(8,128)S(1)} %copy-done.3), channel_id=2, replica_groups=mesh['gx_0'=8,'gx_1'=2,'gy_0'=4,'gy_1'=2,'gy_2'=2] {'gy_0','gy_1','gy_2'}, dimensions={0}, use_global_device_ids=true | all-gather | bytes 278528 | tf_op jit(solution)/shard_map/all_gather | solution.py:65
  34.8 0.7 broadcast_select_fusion
  35.6 65.4 %all-reduce.3.cloned.1.call-done = f32[128,512]{0,1:T(8,128)} async-done(((f32[128,512]{0,1:T(8,128)}), f32[128,512]{0,1:T(8,128)}) %all-reduce.3.cloned.1.call-update) | async-done | bytes 262160 | tf_op jit(solution)/shard_map/psum | solution.py:27
  101.0 0.8 copy-done.2
  101.9 39.7 %all-reduce.5.cloned.1.call-done = f32[128,512]{0,1:T(8,128)} async-done(((f32[128,512]{0,1:T(8,128)}), f32[128,512]{0,1:T(8,128)}) %all-reduce.5.cloned.1.call-update) | async-done | bytes 262160 | tf_op jit(solution)/shard_map/psum | solution.py:27
  141.6 2.1 multiply_reduce_fusion
  143.8 14.6 %psum.51 = f32[]{:T(128)} all-reduce(f32[]{:T(128)} %get-tuple-element.10), channel_id=1, replica_groups=mesh['gx_0'=8,'gx_1'=2,'gy_0'=4,'gy_1'=2,'gy_2'=2] {'gx_0'}, use_global_device_ids=true, to_apply=%region_3.4 | all-reduce | flops 1 | bytes 8 | tf_op jit(solution)/shard_map/psum | solution.py:33
  158.3 4.4 %psum.52 = f32[]{:T(128)} all-reduce(f32[]{:T(128)} %psum.51), channel_id=1, replica_groups=mesh['gx_0'=8,'gx_1'=2,'gy_0'=4,'gy_1'=2,'gy_2'=2] {'gx_1'}, use_global_device_ids=true, to_apply=%region_4.5 | all-reduce | flops 1 | bytes 8 | tf_op jit(solution)/shard_map/psum | solution.py:33
  162.7 9.1 %psum.53 = f32[]{:T(128)} all-reduce(f32[]{:T(128)} %psum.52), channel_id=1, replica_groups=mesh['gx_0'=8,'gx_1'=2,'gy_0'=4,'gy_1'=2,'gy_2'=2] {'gy_0'}, use_global_device_ids=true, to_apply=%region_5.6 | all-reduce | flops 1 | bytes 8 | tf_op jit(solution)/shard_map/psum | solution.py:33
  171.8 5.9 %psum.54 = f32[]{:T(128)} all-reduce(f32[]{:T(128)} %psum.53), channel_id=1, replica_groups=mesh['gx_0'=8,'gx_1'=2,'gy_0'=4,'gy_1'=2,'gy_2'=2] {'gy_1'}, use_global_device_ids=true, to_apply=%region_6.7 | all-reduce | flops 1 | bytes 8 | tf_op jit(solution)/shard_map/psum | solution.py:33
  177.7 11.8 %psum.55 = f32[]{:T(128)} all-reduce(f32[]{:T(128)} %psum.54), channel_id=1, replica_groups=mesh['gx_0'=8,'gx_1'=2,'gy_0'=4,'gy_1'=2,'gy_2'=2] {'gy_2'}, use_global_device_ids=true, to_apply=%region_7.8 | all-reduce | flops 1 | bytes 8 | tf_op jit(solution)/shard_map/psum | solution.py:33
  190.1 0.6 select_subtract_fusion
  190.8 3.9 all_gather.33
  195.9 29.4 %all-gather.11.cloned.1.call-done = f32[2048,128]{0,1:T(8,128)} async-done(((f32[256,128]{0,1:T(8,128)}), f32[2048,128]{0,1:T(8,128)}) %all-gather.11.cloned.1.call-update) | async-done | bytes 1048592 | tf_op jit(solution)/shard_map/all_gather | solution.py:15
  225.2 56.8 %all-gather.9.cloned.1.call-done = f32[128,2048]{0,1:T(8,128)} async-done(((f32[128,128]{0,1:T(8,128)}), f32[128,2048]{0,1:T(8,128)}) %all-gather.9.cloned.1.call-update) | async-done | bytes 1048592 | tf_op jit(solution)/shard_map/all_gather | solution.py:44
  282.0 3.4 fusion.3
  285.4 3.9 all_gather.35
  289.4 44.5 %all-gather.7.cloned.1.call-done = f32[128,2048]{0,1:T(8,128)} async-done(((f32[128,128]{0,1:T(8,128)}), f32[128,2048]{0,1:T(8,128)}) %all-gather.7.cloned.1.call-update) | async-done | bytes 1048592 | tf_op jit(solution)/shard_map/all_gather | solution.py:44
  333.9 33.6 %all-gather.13.cloned.1.call-done = f32[2048,128]{1,0:T(8,128)} async-done(((f32[256,128]{1,0:T(8,128)}), f32[2048,128]{1,0:T(8,128)}) %all-gather.13.cloned.1.call-update) | async-done | bytes 1048592 | tf_op jit(solution)/shard_map/all_gather | solution.py:15
  367.5 4.0 fusion
  371.5 0.7 copy.11
  372.2 53.0 %all-gather.15.cloned.1.call-done = f32[128,2048]{0,1:T(8,128)} async-done(((f32[128,128]{0,1:T(8,128)}), f32[128,2048]{0,1:T(8,128)}) %all-gather.15.cloned.1.call-update) | async-done | bytes 1048592 | tf_op jit(solution)/shard_map/all_gather | solution.py:44
  425.2 3.7 fusion.4
  (24 shorter events, 1.7 us)
Async XLA Ops:
  7.2 0.7 copy-start.3
  7.2 93.8 %all-reduce.3.cloned.1.call-start = ((), (), s32[]{:S(2)}) async-start(), calls=%async_computation | async-start | bytes 524288 | tf_op jit(solution)/shard_map/psum | solution.py:27
  35.6 106.1 %all-reduce.5.cloned.1.call-start = ((), (), s32[]{:S(2)}) async-start(), calls=%async_computation.1 | async-start | bytes 524288 | tf_op jit(solution)/shard_map/psum | solution.py:27
  101.0 0.8 copy-start.2
  101.0 124.2 %all-gather.11.cloned.1.call-start = ((), (), s32[]{:S(2)}) async-start(), calls=%async_computation.4 | async-start | bytes 1179648 | tf_op jit(solution)/shard_map/all_gather | solution.py:15
  190.8 3.9 copy-start.1
  194.7 87.3 %all-gather.9.cloned.1.call-start = ((), (), s32[]{:S(2)}) async-start(), calls=%async_computation.3 | async-start | bytes 1114112 | tf_op jit(solution)/shard_map/all_gather | solution.py:44
  195.2 138.6 %all-gather.7.cloned.1.call-start = ((), (), s32[]{:S(2)}) async-start(), calls=%async_computation.2 | async-start | bytes 1114112 | tf_op jit(solution)/shard_map/all_gather | solution.py:44
  195.8 171.6 %all-gather.13.cloned.1.call-start = ((), (), s32[]{:S(2)}) async-start(), calls=%async_computation.5 | async-start | bytes 1179648 | tf_op jit(solution)/shard_map/all_gather | solution.py:15
  289.3 135.9 %copy-start = (f32[2048,128]{0,1:T(8,128)S(1)}, f32[2048,128]{0,1:T(8,128)}, u32[]{:S(2)}) copy-start(f32[2048,128]{0,1:T(8,128)} %all-gather.11.cloned.1.call-done) | copy-start | bytes 3145732
  289.3 135.9 %all-gather.15.cloned.1.call-start = ((), (), s32[]{:S(2)}) async-start(), calls=%async_computation.6 | async-start | bytes 1114112 | tf_op jit(solution)/shard_map/all_gather | solution.py:44
Sparse Core Ops, SparseCore 0:
  35.7 65.2 all-reduce.2
  103.5 38.0 all-reduce.4
  194.8 30.4 all-gather.10
  228.4 53.5 all-gather.8
  285.2 48.6 all-gather.6
  335.5 31.8 all-gather.12
  371.6 53.5 all-gather.14
